TPU v7x, 32 devices: a whole 2x2x4 slice. The times are simulated.
32 devices in a mesh: grp: 1, exp: 32 (over z, y, x, core).
Axes of the slice: x: 2, y: 2, z: 4, core: 2. Of those that a mesh axis runs over, the one named last changes fastest.
Arguments:
- tokens: bfloat16 [512, 2048], P(('grp', 'exp')), may hold values from -6 to 6
- routed_expert_index: int32 [512, 6], P(('grp', 'exp')), may hold values from 0 to 15, all different within a row; in each aligned block of 16 rows (0 to 15, 16 to 31, ...) at most 8 rows name the same one
- routing_gate_weight: float32 [512, 6], P(('grp', 'exp')), may hold values from 0.05 to 0.5
- token_adapter_index: int32 [512], P('grp'), may hold values from 0 to 511
- gate_weight_pieces: bfloat16 [32, 2048, 704], P('exp'), may hold values from -0.125 to 0.125
- up_weight: bfloat16 [32, 2048, 704], P('exp'), may hold values from -0.125 to 0.125
- down_weight: bfloat16 [32, 704, 2048], P('exp'), may hold values from -0.15625 to 0.15625
- adapter_down_matrix: bfloat16 [2048, 8192], P('exp'), may hold values from -0.125 to 0.125
- adapter_up_matrix: bfloat16 [2048, 8192], P('exp'), may hold values from -1.5 to 1.5
Outputs:
- mixed: bfloat16 [512, 2048], P(('grp', 'exp'))
Inputs may be any that keep to these rules, and one draw needn't show every extreme that they name: `routed_expert_index`: each token names 6 different experts; among the 16 tokens of one index of exp (aligned blocks of rows) no expert is named more than 8 times.
All inputs are finite; a program needn't handle non-finite values.
Results may differ from a plain program's by a relative error of at most 0.009.
Values may be sent and summed in bfloat16 or wider, within the bound.
A program may use at most 128 MiB of HBM per device.

v0:
```python
import jax
import jax.numpy as jnp
from jax import lax
from jax.sharding import PartitionSpec as P

TOP = 6
ADAPTER_RANK = 16


def expert_half(row_block, gate_weight_pieces, up_weight, down_weight):
    gate_act = jnp.dot(row_block, gate_weight_pieces[0], preferred_element_type=jnp.float32)
    up_act = jnp.dot(row_block, up_weight[0], preferred_element_type=jnp.float32)
    hidden = (jax.nn.silu(gate_act) * up_act).astype(jnp.bfloat16)
    return jnp.dot(hidden, down_weight[0], preferred_element_type=jnp.float32)


def per_device(
    tokens,
    routed_expert_index,
    routing_gate_weight,
    token_adapter_index,
    gate_weight_pieces,
    up_weight,
    down_weight,
    adapter_down_matrix,
    adapter_up_matrix,
):
    devices = lax.axis_size("exp")
    experts = devices // 2
    tok_dev = tokens.shape[0]
    model_width = tokens.shape[1]
    capacity = 2 * (tok_dev * TOP // devices + 1)
    flat_ids = routed_expert_index.reshape(-1)
    gate_col = routing_gate_weight.reshape(-1, 1)
    one_hot = (flat_ids[:, None] == jnp.arange(experts, dtype=jnp.int32)[None, :]).astype(jnp.int32)
    counted = jnp.cumsum(one_hot, axis=0)
    position = jnp.sum(one_hot * counted, axis=1) - 1
    slots = flat_ids * capacity + position
    token_rows = jnp.repeat(tokens, TOP, axis=0)
    buffer = jnp.zeros((experts * capacity, model_width), tokens.dtype).at[slots].set(token_rows)
    buffer, slots = (buffer, slots)
    doubled = jnp.broadcast_to(
        buffer.reshape(experts, 1, capacity, model_width), (experts, 2, capacity, model_width)
    )
    doubled = doubled.reshape(devices, capacity, model_width)
    received = lax.all_to_all(doubled, "exp", split_axis=0, concat_axis=0, tiled=True)
    sources = received.shape[0]
    items = received.shape[1]
    output = expert_half(
        received.reshape(sources * items, model_width), gate_weight_pieces, up_weight, down_weight
    )
    partial_value = output.reshape(sources, items, model_width)
    returned = lax.all_to_all(
        partial_value.astype(jnp.bfloat16), "exp", split_axis=0, concat_axis=0, tiled=True
    ).astype(partial_value.dtype)
    results = jnp.sum(returned.reshape(experts, 2, capacity, model_width), axis=1)
    gather_results = results.reshape(experts * capacity, model_width)
    picked = gather_results[slots] * gate_col
    routed = jnp.sum(picked.reshape(tok_dev, TOP, model_width), axis=1)
    columns = lax.all_to_all(tokens, "exp", split_axis=1, concat_axis=0, tiled=True)
    feature_rows = adapter_down_matrix.shape[0]
    adapter_table = adapter_down_matrix.shape[1] // ADAPTER_RANK
    down_selected = adapter_down_matrix.reshape(feature_rows, adapter_table, ADAPTER_RANK)[
        :, token_adapter_index, :
    ]
    rank_terms = jnp.einsum(
        "tf,ftr->tr", columns, down_selected, preferred_element_type=jnp.float32
    )
    gathered_ranks = lax.psum(rank_terms, "exp").astype(jnp.bfloat16)
    up_selected = adapter_up_matrix.reshape(feature_rows, adapter_table, ADAPTER_RANK)[
        :, token_adapter_index, :
    ]
    correction_cols = jnp.einsum(
        "tr,ftr->tf", gathered_ranks, up_selected, preferred_element_type=jnp.float32
    )
    lowrank_delta = lax.all_to_all(
        correction_cols.astype(jnp.bfloat16), "exp", split_axis=0, concat_axis=1, tiled=True
    )
    return (routed + lowrank_delta.astype(jnp.float32)).astype(jnp.bfloat16)


def solution(mesh):
    placed = (
        P(("grp", "exp"), None),
        P(("grp", "exp"), None),
        P(("grp", "exp"), None),
        P("grp"),
        P("exp", None, None),
        P("exp", None, None),
        P("exp", None, None),
        P("exp", None),
        P("exp", None),
    )
    return jax.shard_map(
        per_device, mesh=mesh, in_specs=placed, out_specs=P(("grp", "exp"), None), check_vma=False
    )
```

profile of v0, /device:TPU:0, one launch (start us, length us, event | category | flops | bytes accessed | tf_op | source)
XLA Modules:
  0.0 140.4 jit_solution(14712672242584712208)
XLA Ops:
  0.0 1.2 all_to_all.32
  1.2 0.1 copy.38
  1.2 0.8 reshape.132
  2.0 7.3 %all-to-all-start.2 = ((bf16[32,2,512]{2,1,0:T(2,128)(2,1)}), bf16[32,2,512]{2,1,0:T(2,128)(2,1)S(1)}, u32[]{:S(2)}, u32[]{:S(2)}) async-start(bf16[32,2,512]{2,1,0:T(2,128)(2,1)} %reshape.132), calls=%async_computation.2 | async-start | bytes 131072 | tf_op jit(solution)/shard_map/all_to_all | solution.py:60
  9.3 0.7 broadcast_multiply_fusion
  10.0 0.8 copy.22
  10.8 0.1 copy.21
  10.9 0.1 mul.37
  11.0 0.1 eq.15
  11.1 0.1 fusion.26
  11.2 0.1 reduce_window_sum.11
  11.3 0.2 select_reduce_fusion
  11.5 0.9 broadcast_in_dim.21
  12.4 0.9 reshape.119
  13.3 1.8 %scatter_custom_fusion = bf16[128,2048]{1,0:T(8,128)(2,1)S(1)} fusion(s32[96]{0:T(128)S(1)} %fusion.27, bf16[96,2048]{1,0:T(8,128)(2,1)} %reshape.119, bf16[]{:T(256)} %constant.8.clone.1), kind=kCustom, calls=%fused_computation.25 | custom fusion | bytes 524800 | tf_op jit(solution)/shard_map/scatter | solution.py:40
  15.1 1.7 %all-to-all-done.2 = bf16[32,2,512]{2,1,0:T(2,128)(2,1)S(1)} async-done(((bf16[32,2,512]{2,1,0:T(2,128)(2,1)}), bf16[32,2,512]{2,1,0:T(2,128)(2,1)S(1)}, u32[]{:S(2)}, u32[]{:S(2)}) %all-to-all-start.2) | async-done | bytes 65568 | tf_op jit(solution)/shard_map/all_to_all | solution.py:60
  16.8 1.1 broadcast_in_dim.23
  17.9 4.3 %all-to-all-start = ((bf16[32,8,2048]{2,1,0:T(8,128)(2,1)}), bf16[32,8,2048]{2,1,0:T(8,128)(2,1)}, u32[]{:S(2)}, u32[]{:S(2)}) async-start(bf16[32,8,2048]{2,1,0:T(8,128)(2,1)} %bitcast.67), calls=%async_computation | async-start | bytes 2097152 | tf_op jit(solution)/shard_map/all_to_all | solution.py:46
  22.1 0.0 copy-start.2
  22.2 2.8 %copy.25 = bf16[64,8192]{0,1:T(8,128)(2,1)} copy(bf16[64,8192]{1,0:T(8,128)(2,1)} %param.16) | data formatting | bytes 2097152 | tf_op args[7]
  24.9 2.8 %copy.27 = bf16[64,8192]{0,1:T(8,128)(2,1)} copy(bf16[64,8192]{1,0:T(8,128)(2,1)} %param.17) | data formatting | bytes 2097152 | tf_op args[8]
  27.7 3.9 %gather_fusion.1 = bf16[512,64,16]{1,2,0:T(8,128)(2,1)} fusion(bf16[64,512,16]{0,2,1:T(8,128)(2,1)} %bitcast.65, s32[1024]{0:T(1024)S(1)} %pad_clamp_fusion), kind=kCustom, calls=%fused_computation.1 | custom fusion | bytes 2099200 | tf_op jit(solution)/shard_map/gather | solution.py:63
  31.6 4.0 %gather_fusion.2 = bf16[512,64,16]{1,2,0:T(8,128)(2,1)} fusion(bf16[64,512,16]{0,2,1:T(8,128)(2,1)} %bitcast.64, s32[1024]{0:T(1024)S(1)} %pad_clamp_fusion), kind=kCustom, calls=%fused_computation.2 | custom fusion | bytes 2099200 | tf_op jit(solution)/shard_map/gather | solution.py:70
  35.6 0.1 reshape.133
  35.8 2.8 %fusion.11 = f32[512,1,16]{2,1,0:T(1,128)S(1)} fusion(bf16[512,64,16]{1,2,0:T(8,128)(2,1)} %gather_fusion.1, bf16[512,64,1]{1,0,2:T(8,128)(2,1)S(1)} %bitcast.74), kind=kOutput, calls=%fused_computation.14 | convolution fusion | flops 1048576 | bytes 1146880 | tf_op jit(solution)/shard_map/tf,ftr->tr/dot_general | solution.py:66
  38.5 43.0 %psum.7 = bf16[512,16]{1,0:T(8,128)(2,1)S(1)} all-reduce(f32[512,16]{1,0:T(8,128)S(1)} %bitcast.71), channel_id=1, replica_groups=mesh['grp'=1,'exp'=32] {'exp'}, use_global_device_ids=true, to_apply=%region_5.6 | all-reduce | flops 8192 | bytes 49152 | tf_op jit(solution)/shard_map/psum | solution.py:69
  81.6 2.3 %fusion.9 = f32[512,1,64]{2,1,0:T(1,128)S(1)} fusion(bf16[512,64,16]{1,2,0:T(8,128)(2,1)} %gather_fusion.2, bf16[512,16,1]{1,0,2:T(8,128)(2,1)S(1)} %bitcast.73), kind=kOutput, calls=%fused_computation.12 | convolution fusion | flops 1048576 | bytes 1196032 | tf_op jit(solution)/shard_map/tr,ftr->tf/dot_general | solution.py:73
  83.9 0.8 reshape.134
  84.6 0.0 all-to-all-done
  84.6 3.9 %all-to-all-start.3 = ((bf16[32,2,512]{2,1,0:T(2,128)(2,1)}), bf16[32,2,512]{2,1,0:T(2,128)(2,1)S(1)}, u32[]{:S(2)}, u32[]{:S(2)}) async-start(bf16[32,2,512]{2,1,0:T(2,128)(2,1)} %reshape.134), calls=%async_computation.3 | async-start | bytes 131072 | tf_op jit(solution)/shard_map/all_to_all | solution.py:76
  88.5 0.0 copy-start.3
  88.5 3.2 %fusion.4 = f32[256,704]{0,1:T(8,128)S(1)} fusion(bf16[1,2048,704]{1,2,0:T(8,128)(2,1)} %param.13, bf16[32,8,2048]{2,1,0:T(8,128)(2,1)} %all-to-all-done), kind=kOutput, calls=%fused_computation.8 | convolution fusion | flops 738197504 | bytes 4653056 | tf_op jit(solution)/shard_map/dot_general | solution.py:11
  91.8 2.9 %fusion.16 = bf16[256,704]{0,1:T(8,128)(2,1)} fusion(bf16[1,2048,704]{1,2,0:T(8,128)(2,1)S(1)} %copy-done.3, bf16[32,8,2048]{2,1,0:T(8,128)(2,1)} %all-to-all-done, f32[256,704]{0,1:T(8,128)S(1)} %fusion.4), kind=kOutput, calls=%fused_computation.17 | convolution fusion | flops 739278848 | bytes 5013504 | tf_op jit(solution)/shard_map/dot_general | solution.py:12
  94.7 1.2 copy.23
  95.8 0.0 copy-start.1
  95.9 2.0 %fusion.6 = bf16[32,8,2048]{2,1,0:T(8,128)(2,1)} fusion(bf16[1,704,2048]{2,1,0:T(8,128)(2,1)S(1)} %copy-done, bf16[256,704]{1,0:T(8,128)(2,1)S(1)} %copy.23), kind=kOutput, calls=%fused_computation.10 | convolution fusion | flops 738721792 | bytes 4292608 | tf_op jit(solution)/shard_map/dot_general | solution.py:14
  97.9 0.0 all-to-all-done.3
  97.9 6.0 %all-to-all-start.1 = ((bf16[32,8,2048]{2,1,0:T(8,128)(2,1)}), bf16[32,8,2048]{2,1,0:T(8,128)(2,1)}, u32[]{:S(2)}, u32[]{:S(2)}) async-start(bf16[32,8,2048]{2,1,0:T(8,128)(2,1)} %fusion.6), calls=%async_computation.1 | async-start | bytes 2097152 | tf_op jit(solution)/shard_map/all_to_all | solution.py:53
  103.9 0.1 copy.24
  104.0 0.1 reshape.135
  104.1 0.1 copy.28
  104.2 0.1 reshape.90
  104.3 25.7 %all-to-all-done.1 = bf16[32,8,2048]{2,1,0:T(8,128)(2,1)} async-done(((bf16[32,8,2048]{2,1,0:T(8,128)(2,1)}), bf16[32,8,2048]{2,1,0:T(8,128)(2,1)}, u32[]{:S(2)}, u32[]{:S(2)}) %all-to-all-start.1) | async-done | bytes 1048608 | tf_op jit(solution)/shard_map/all_to_all | solution.py:53
  130.0 2.5 %convert_reduce_fusion = f32[16,8,2048]{2,1,0:T(8,128)} fusion(bf16[32,8,2048]{2,1,0:T(8,128)(2,1)} %all-to-all-done.1), kind=kLoop, calls=%fused_computation.11 | loop fusion | flops 786432 | bytes 2097152 | tf_op jit(solution)/shard_map/reduce_sum | solution.py:56
  132.6 3.3 %gather_fusion = f32[96,2048]{1,0:T(8,128)} fusion(f32[128,2048]{1,0:T(8,128)} %bitcast.66, s32[1024]{0:T(1024)S(1)} %pad_clamp_fusion.1), kind=kCustom, calls=%fused_computation | custom fusion | bytes 1573248 | tf_op jit(solution)/shard_map/gather | solution.py:58
  135.9 2.2 %gather.12 = f32[16,6,2048]{2,1,0:T(8,128)} reshape(f32[96,2048]{1,0:T(8,128)} %gather_fusion) | data formatting | bytes 1572864 | tf_op jit(solution)/shard_map/gather | solution.py:58
  138.1 1.6 %multiply_reduce_fusion = f32[16,2048]{1,0:T(8,128)S(1)} fusion(f32[16,6,2048]{2,1,0:T(8,128)} %gather.12, f32[16,6]{1,0:T(8,128)S(1)} %copy.24), kind=kLoop, calls=%fused_computation.20 | loop fusion | flops 360448 | bytes 917888 | tf_op jit(solution)/shard_map/reduce_sum | solution.py:59
  139.7 0.6 add_convert_fusion
  (11 shorter events, 0.1 us)
Async XLA Ops:
  0.0 95.8 %copy-start = (bf16[1,704,2048]{2,1,0:T(8,128)(2,1)S(1)}, bf16[1,704,2048]{2,1,0:T(8,128)(2,1)}, u32[]{:S(2)}) copy-start(bf16[1,704,2048]{2,1,0:T(8,128)(2,1)} %param.15) | copy-start | bytes 8650756
  2.0 14.7 %all-to-all-start.2 = ((bf16[32,2,512]{2,1,0:T(2,128)(2,1)}), bf16[32,2,512]{2,1,0:T(2,128)(2,1)S(1)}, u32[]{:S(2)}, u32[]{:S(2)}) async-start(bf16[32,2,512]{2,1,0:T(2,128)(2,1)} %reshape.132), calls=%async_computation.2 | async-start | bytes 131072 | tf_op jit(solution)/shard_map/all_to_all | solution.py:60
  17.9 66.8 %all-to-all-start = ((bf16[32,8,2048]{2,1,0:T(8,128)(2,1)}), bf16[32,8,2048]{2,1,0:T(8,128)(2,1)}, u32[]{:S(2)}, u32[]{:S(2)}) async-start(bf16[32,8,2048]{2,1,0:T(8,128)(2,1)} %bitcast.67), calls=%async_computation | async-start | bytes 2097152 | tf_op jit(solution)/shard_map/all_to_all | solution.py:46
  22.1 5.6 %copy-start.2 = (s32[512]{0:T(512)S(1)}, s32[512]{0:T(512)}, u32[]{:S(2)}) copy-start(s32[512]{0:T(512)} %param.12) | copy-start | bytes 6148
  84.6 13.3 %all-to-all-start.3 = ((bf16[32,2,512]{2,1,0:T(2,128)(2,1)}), bf16[32,2,512]{2,1,0:T(2,128)(2,1)S(1)}, u32[]{:S(2)}, u32[]{:S(2)}) async-start(bf16[32,2,512]{2,1,0:T(2,128)(2,1)} %reshape.134), calls=%async_computation.3 | async-start | bytes 131072 | tf_op jit(solution)/shard_map/all_to_all | solution.py:76
  88.5 3.3 %copy-start.3 = (bf16[1,2048,704]{1,2,0:T(8,128)(2,1)S(1)}, bf16[1,2048,704]{1,2,0:T(8,128)(2,1)}, u32[]{:S(2)}) copy-start(bf16[1,2048,704]{1,2,0:T(8,128)(2,1)} %param.14) | copy-start | bytes 8650756
  95.8 8.0 %copy-start.1 = (f32[16,6]{0,1:T(8,128)S(1)}, f32[16,6]{0,1:T(8,128)}, u32[]{:S(2)}) copy-start(f32[16,6]{0,1:T(8,128)} %param.11) | copy-start | bytes 1156
  97.9 32.1 %all-to-all-start.1 = ((bf16[32,8,2048]{2,1,0:T(8,128)(2,1)}), bf16[32,8,2048]{2,1,0:T(8,128)(2,1)}, u32[]{:S(2)}, u32[]{:S(2)}) async-start(bf16[32,8,2048]{2,1,0:T(8,128)(2,1)} %fusion.6), calls=%async_computation.1 | async-start | bytes 2097152 | tf_op jit(solution)/shard_map/all_to_all | solution.py:53
where the time goes:
time: 141 us; the launch traced here: 140 us
  blocking collectives  43 us (30%)
  local copies, waits for them, and re-layouts  29.2 us (21%)
  waiting for transfers between devices  27.4 us (19%)
  starting transfers between devices  21.4 us (15%)
  matrix products  13.2 us (9%)
  other arithmetic  5.94 us (4%)
    psum x1, blocking collectives, per_device(): gathered_ranks = lax.psum(rank_terms, 'exp').astype(jnp.bfloat16)  43 us
    all_to_all x1, waiting for transfers between devices, per_device(): lax.all_to_all(partial_value.astype(jnp.bfloat16), 'exp', split_axis=0, c...  25.7 us
    unnamed x16, local copies, waits for them, and re-layouts  8.22 us
    all_to_all x1, starting transfers between devices, per_device(): lax.all_to_all(tokens, 'exp', split_axis=1, concat_axis=0, tiled=True)  7.33 us
    all_to_all x1, starting transfers between devices, per_device(): lax.all_to_all(partial_value.astype(jnp.bfloat16), 'exp', split_axis=0, c...  5.96 us
    gather x2, local copies, waits for them, and re-layouts, per_device(): picked = gather_results[slots] * gate_col  5.55 us
    all_to_all x1, starting transfers between devices, per_device(): lax.all_to_all(doubled, 'exp', split_axis=0, concat_axis=0, tiled=True)  4.27 us
    gather x1, local copies, waits for them, and re-layouts, per_device(): adapter_up_matrix.reshape(feature_rows, adapter_table, ADAPTER_RANK)  3.97 us
  transfers between devices with their start and end apart: 4, of which 2 were waited for; matrix products, arithmetic and copies ran while one was open for 25% of the time, Pallas kernels for 0%

commit v1 on v0

v1 whole, which is shorter than its diff:
```python
import functools

import jax
import jax.numpy as jnp
from jax import lax
from jax.experimental import pallas as pl
from jax.experimental.pallas import tpu as pltpu
from jax.sharding import PartitionSpec as P

RANK = 16
LANES = 128
BF16 = jnp.bfloat16
F32 = jnp.float32
MESH = pl.DeviceIdType.MESH


def kernel(
    chips, cap, top, x_ref, idx_ref, gate_ref, aid_ref, wg_hbm, wu_hbm, wd_hbm, adn_hbm, aup_hbm, out_ref,
    wg, wu, wd, adn, aup, col, disp, recv_a, recv_b, xs, hid, y_own, sib_send, sib_recv,
    rs_send, rs_recv, ag, cor_send, cor_recv, ret_send, ret_recv, low,
    w_sem, adl_sem, ad_s, ad_r, col_s, col_r, disp_s, disp_r, fwd_s, fwd_r, rs_s, rs_r,
    ag_s, ag_r, cor_s, cor_r, ret_s, ret_r, sib_s, sib_r,
):
    me = lax.axis_index("exp")
    q = lax.div(me, 2)
    c = lax.rem(me, 2)
    sib = me + 1 - 2 * c
    rows, width = x_ref.shape
    feats = adn_hbm.shape[0]
    bank = adn_hbm.shape[1]
    group = chips * rows
    slots = chips * cap
    off = pl.multiple_of(lax.rem(me * feats, LANES), feats)

    def remote(src, dst, ss, rs, dev):
        return pltpu.make_async_remote_copy(
            src_ref=src, dst_ref=dst, send_sem=ss, recv_sem=rs, device_id={"exp": dev}, device_id_type=MESH
        )

    def peer(r):
        return lax.rem(q + r, chips)

    def source(r):
        return lax.rem(q + chips - r, chips)

    def others(fn):
        def step(r, carry):
            fn(r)
            return carry

        lax.fori_loop(1, chips, step, 0)

    barrier = pltpu.get_barrier_semaphore()
    if 2 * feats < LANES:
        adn[...] = jnp.zeros_like(adn)
        aup[...] = jnp.zeros_like(aup)
    others(lambda r: pl.semaphore_signal(barrier, inc=1, device_id={"exp": 2 * peer(r) + c}, device_id_type=MESH))
    pl.semaphore_signal(barrier, inc=1, device_id={"exp": sib}, device_id_type=MESH)

    own_rows = pl.ds(off, feats)
    local = [
        pltpu.make_async_copy(adn_hbm, adn.at[own_rows], adl_sem.at[0]),
        pltpu.make_async_copy(wg_hbm.at[0], wg, w_sem.at[0]),
        pltpu.make_async_copy(wu_hbm.at[0], wu, w_sem.at[1]),
        pltpu.make_async_copy(aup_hbm, aup.at[own_rows], adl_sem.at[1]),
        pltpu.make_async_copy(wd_hbm.at[0], wd, w_sem.at[2]),
    ]
    for cp in local:
        cp.start()

    lane = lax.broadcasted_iota(jnp.int32, (rows, slots), 1)
    lane_e = lax.div(lane, cap)
    chosen = jnp.zeros((rows, slots), F32)
    weight = jnp.zeros((rows, slots), F32)
    for k in range(top):
        hit = idx_ref[:, k : k + 1] == lane_e
        chosen = chosen + jnp.where(hit, 1.0, 0.0)
        weight = weight + jnp.where(hit, gate_ref[:, k : k + 1], 0.0)
    lower = jnp.where(
        lax.broadcasted_iota(jnp.int32, (rows, rows), 1) < lax.broadcasted_iota(jnp.int32, (rows, rows), 0), 1.0, 0.0
    )
    rank_of = jnp.dot(lower.astype(BF16), chosen.astype(BF16), preferred_element_type=F32)
    slot_p = lax.rem(lane, cap).astype(F32)
    pick = jnp.where((chosen > 0.5) & (rank_of == slot_p), 1.0, 0.0)
    combine = pick * weight
    packed = jnp.dot(pick.T.astype(BF16), x_ref[...], preferred_element_type=F32)
    disp[...] = packed.reshape(chips, cap, width).astype(BF16)
    recv_a[pl.ds(q, 1)] = disp[pl.ds(q, 1)]

    def lanes_of(chip):
        return pl.ds(pl.multiple_of(lax.div(chip * 2 * feats, LANES) * LANES, LANES), LANES)

    col[pl.ds(q, 1)] = x_ref[:, lanes_of(q)].reshape(1, rows, LANES)

    pl.semaphore_wait(barrier, chips)

    def col_copy(to, slot):
        return remote(x_ref.at[:, lanes_of(to)], col.at[slot], col_s.at[to], col_r.at[slot], 2 * to + c)

    def disp_copy(to, slot):
        return remote(disp.at[to], recv_a.at[slot], disp_s.at[to], disp_r.at[slot], 2 * to + c)

    def fwd_copy(block):
        return remote(recv_a.at[block], recv_b.at[block], fwd_s.at[block], fwd_r.at[block], sib)

    def rs_copy(to, slot):
        return remote(rs_send.at[to], rs_recv.at[slot], rs_s.at[to], rs_r.at[slot], 2 * to + c)

    def ag_copy(to, slot):
        return remote(low, ag.at[slot], ag_s.at[to], ag_r.at[slot], 2 * to + c)

    def cor_copy(to, slot):
        return remote(cor_send.at[to], cor_recv.at[slot], cor_s.at[to], cor_r.at[slot], 2 * to + c)

    def ret_copy(to, slot):
        return remote(ret_send.at[to], ret_recv.at[slot], ret_s.at[to], ret_r.at[slot], 2 * to + c)

    others(lambda r: col_copy(peer(r), q).start())
    adn_copy = remote(adn_hbm, adn.at[own_rows], ad_s.at[0], ad_r.at[0], sib)
    aup_copy = remote(aup_hbm, aup.at[own_rows], ad_s.at[1], ad_r.at[1], sib)
    adn_copy.start()
    others(lambda r: disp_copy(peer(r), q).start())
    aup_copy.start()
    fwd_copy(q).start()

    part = lax.broadcasted_iota(jnp.int32, (chips, rows, 2 * rows), 2)
    row = lax.broadcasted_iota(jnp.int32, (chips, rows, 2 * rows), 1)
    spread = jnp.broadcast_to(aid_ref[...].astype(F32)[:, None, :], (chips, rows, 2 * rows))
    ids = jnp.sum(jnp.where(part == row + c * rows, spread, 0.0), axis=2, keepdims=True)
    ids = jnp.broadcast_to(ids, (chips, rows, LANES)).reshape(group, LANES).astype(jnp.int32)
    per = LANES // RANK
    id_hi = lax.div(ids, per)
    id_lo = ids - id_hi * per
    lane_g = lax.broadcasted_iota(jnp.int32, (group, LANES), 1)
    keep = lax.div(lane_g, RANK) == id_lo

    others(lambda r: col_copy(q, source(r)).wait_recv())
    local[0].wait()
    adn_copy.wait_recv()
    cols = col[...].reshape(group, LANES)
    span = 512
    sub = span // LANES

    def down_step(i, acc):
        at = pl.multiple_of(i * span, span)
        h = jnp.dot(cols, adn[:, pl.ds(at, span)], preferred_element_type=F32)
        for s in range(sub):
            acc = jnp.where(id_hi == i * sub + s, h[:, s * LANES : (s + 1) * LANES], acc)
        return acc

    terms = lax.fori_loop(0, bank // span, down_step, jnp.zeros((group, LANES), F32))
    terms = jnp.where(keep, terms, 0.0).astype(BF16)
    fi = lax.broadcasted_iota(jnp.int32, (LANES, LANES), 0)
    fj = lax.broadcasted_iota(jnp.int32, (LANES, LANES), 1)
    fold = jnp.where(lax.rem(fi, RANK) == lax.rem(fj, RANK), 1.0, 0.0).astype(BF16)
    folded = jnp.dot(terms, fold, preferred_element_type=F32).astype(BF16)
    rs_send[...] = folded.reshape(chips, rows, LANES)
    rs_recv[pl.ds(q, 1)] = rs_send[pl.ds(q, 1)]
    others(lambda r: rs_copy(peer(r), q).start())

    def forward(r):
        disp_copy(q, source(r)).wait_recv()
        fwd_copy(source(r)).start()

    others(forward)

    others(lambda r: rs_copy(q, source(r)).wait_recv())
    low[...] = jnp.sum(rs_recv[...].astype(F32), axis=0).astype(BF16)
    ag[pl.ds(q, 1)] = low[...].reshape(1, rows, LANES)
    others(lambda r: ag_copy(peer(r), q).start())

    ksplit = 512
    nsplit = 512
    half = wd.shape[0]

    def load_rows(ref):
        xs[...] = ref[...].astype(F32).reshape(slots, width).astype(BF16)

    def hidden():
        def step(i, accs):
            at = pl.multiple_of(i * ksplit, ksplit)
            xk = xs[:, pl.ds(at, ksplit)]
            return (
                accs[0] + jnp.dot(xk, wg[pl.ds(at, ksplit), :], preferred_element_type=F32),
                accs[1] + jnp.dot(xk, wu[pl.ds(at, ksplit), :], preferred_element_type=F32),
            )

        zero = jnp.zeros((slots, half), F32)
        g, u = lax.fori_loop(0, width // ksplit, step, (zero, zero))
        hid[...] = (g / (1.0 + jnp.exp(-g)) * u).astype(BF16)

    load_rows(recv_a)
    local[1].wait()
    local[2].wait()
    hidden()
    local[4].wait()

    def own_step(i, carry):
        at = pl.ds(pl.multiple_of(i * nsplit, nsplit), nsplit)
        y_own[:, at] = jnp.dot(hid[...], wd[:, at], preferred_element_type=F32)
        return carry

    lax.fori_loop(0, width // nsplit, own_step, 0)

    fwd_in = lambda block: fwd_copy(block).wait_recv()
    fwd_in(q)
    others(lambda r: fwd_in(source(r)))
    load_rows(recv_b)
    hidden()

    def sib_step(i, carry):
        at = pl.ds(pl.multiple_of(i * nsplit, nsplit), nsplit)
        y = jnp.dot(hid[...], wd[:, at], preferred_element_type=F32)
        sib_send[:, :, at] = y.reshape(chips, cap, nsplit).astype(BF16)
        return carry

    lax.fori_loop(0, width // nsplit, sib_step, 0)
    sib_copy = remote(sib_send, sib_recv, sib_s.at[0], sib_r.at[0], sib)
    sib_copy.start()

    others(lambda r: ag_copy(q, source(r)).wait_recv())
    local[3].wait()
    aup_copy.wait_recv()
    ranks = jnp.where(keep, ag[...].reshape(group, LANES).astype(F32), 0.0)

    def up_step(i, acc):
        at = pl.multiple_of(i * span, span)
        wide = jnp.concatenate([jnp.where(id_hi == i * sub + s, ranks, 0.0).astype(BF16) for s in range(sub)], axis=1)
        return acc + lax.dot_general(
            wide, aup[:, pl.ds(at, span)], (((1,), (1,)), ((), ())), preferred_element_type=F32
        )

    corr = lax.fori_loop(0, bank // span, up_step, jnp.zeros((group, LANES), F32))
    cor_send[...] = corr.astype(BF16).reshape(chips, rows, LANES)
    cor_recv[pl.ds(q, 1)] = cor_send[pl.ds(q, 1)]
    others(lambda r: cor_copy(peer(r), q).start())

    sib_copy.wait_recv()
    ret_send[...] = (y_own[...].reshape(chips, cap, width) + sib_recv[...].astype(F32)).astype(BF16)
    ret_recv[pl.ds(q, 1)] = ret_send[pl.ds(q, 1)]
    others(lambda r: ret_copy(peer(r), q).start())

    others(lambda r: cor_copy(q, source(r)).wait_recv())
    others(lambda r: ret_copy(q, source(r)).wait_recv())
    back = ret_recv[...].astype(F32).reshape(slots, width).astype(BF16)
    c_hi = combine.astype(BF16)
    c_lo = (combine - c_hi.astype(F32)).astype(BF16)
    routed = jnp.dot(c_hi, back, preferred_element_type=F32) + jnp.dot(c_lo, back, preferred_element_type=F32)
    share = LANES // (2 * feats)
    for j in range(width // LANES):
        delta = cor_recv[j * share].astype(F32)
        for s in range(1, share):
            delta = delta + cor_recv[j * share + s].astype(F32)
        at = slice(j * LANES, (j + 1) * LANES)
        out_ref[:, at] = (routed[:, at] + delta).astype(BF16)

    adn_copy.wait_send()
    aup_copy.wait_send()
    sib_copy.wait_send()
    fwd_copy(q).wait_send()

    def drain(r):
        to = peer(r)
        for cp in (col_copy, disp_copy, rs_copy, ag_copy, cor_copy, ret_copy):
            cp(to, q).wait_send()
        fwd_copy(source(r)).wait_send()

    others(drain)


def per_device(tokens, idx, gates, aid, wg, wu, wd, adn, aup):
    devices = lax.axis_size("exp")
    chips = devices // 2
    rows, width = tokens.shape
    top = idx.shape[1]
    half = wd.shape[1]
    feats, bank = adn.shape
    need = 2 * (rows * top // devices + 1)
    cap = -(-need // 8) * 8
    slots = chips * cap
    group = chips * rows
    blocks = lambda *s: pltpu.VMEM(s, BF16)
    sems = lambda n: pltpu.SemaphoreType.DMA((n,))
    vm = pl.BlockSpec(memory_space=pltpu.VMEM)
    hbm = pl.BlockSpec(memory_space=pl.ANY)
    return pl.pallas_call(
        functools.partial(kernel, chips, cap, top),
        out_shape=jax.ShapeDtypeStruct((rows, width), BF16),
        in_specs=[vm, vm, vm, vm, hbm, hbm, hbm, hbm, hbm],
        out_specs=vm,
        scratch_shapes=[
            blocks(width, half), blocks(width, half), blocks(half, width),
            blocks(LANES, bank), blocks(LANES, bank),
            blocks(chips, rows, LANES),
            blocks(chips, cap, width), blocks(chips, cap, width), blocks(chips, cap, width),
            blocks(slots, width), blocks(slots, half), pltpu.VMEM((slots, width), F32),
            blocks(chips, cap, width), blocks(chips, cap, width),
            blocks(chips, rows, LANES), blocks(chips, rows, LANES), blocks(chips, rows, LANES),
            blocks(chips, rows, LANES), blocks(chips, rows, LANES),
            blocks(chips, cap, width), blocks(chips, cap, width), blocks(rows, LANES),
            sems(3), sems(2), sems(2), sems(2),
            *[sems(chips) for _ in range(14)],
            sems(1), sems(1),
        ],
        compiler_params=pltpu.CompilerParams(
            collective_id=0, has_side_effects=True, vmem_limit_bytes=60 * 1024 * 1024
        ),
    )(tokens, idx, gates, aid.reshape(chips, 2 * rows), wg, wu, wd, adn, aup)


def solution(mesh):
    placed = (
        P(("grp", "exp"), None),
        P(("grp", "exp"), None),
        P(("grp", "exp"), None),
        P("grp"),
        P("exp", None, None),
        P("exp", None, None),
        P("exp", None, None),
        P("exp", None),
        P("exp", None),
    )
    return jax.shard_map(
        per_device, mesh=mesh, in_specs=placed, out_specs=P(("grp", "exp"), None), check_vma=False
    )
```

time: 141 us -> 61.8 us (0.44)
  Pallas kernels: 0 us -> 47.5 us
  blocking collectives: 43 us -> 0 us
  waiting for transfers between devices: 27.4 us -> 0 us
  starting transfers between devices: 21.4 us -> 0 us
  local copies, waits for them, and re-layouts: 29.2 us -> 13.1 us
  matrix products: 13.2 us -> 0 us
  other arithmetic: 5.94 us -> 0 us
    pallas_call x0 -> x1, Pallas kernels: none -> 47.5 us  [per_device(): pl.pallas_call(functools.partial(kernel, chips, cap, top), out_shape=jax....]
    psum x1 -> x0, blocking collectives: 43 us -> none  [per_device(): gathered_ranks = lax.psum(rank_terms, 'exp').astype(jnp.bfloat16)]
    all_to_all x4 -> x0, waiting for transfers between devices: 27.4 us -> none  [the longest x1 25.7 us: per_device(): lax.all_to_all(partial_value.astype(jnp.bfloat16), 'exp', split_axis=0, c...]
    all_to_all x4 -> x0, starting transfers between devices: 21.4 us -> none  [the longest x1 7.33 us: per_device(): lax.all_to_all(tokens, 'exp', split_axis=1, concat_axis=0, tiled=True)]
    gather x4 -> x0, local copies, waits for them, and re-layouts: 13.5 us -> none  [the longest x2 5.55 us: per_device(): picked = gather_results[slots] * gate_col]
    dot_general x5 -> x0, matrix products: 13.2 us -> none  [the longest x1 3.23 us: expert_half(): jnp.dot(row_block, gate_weight_pieces[0], preferred_element_type=jnp.floa...]
    reduce_sum x3 -> x0, other arithmetic: 4.32 us -> none  [the longest x1 2.53 us: per_device(): jnp.sum(returned.reshape(experts, 2, capacity, model_width), axis=1)]
    unnamed x16 -> x7, local copies, waits for them, and re-layouts: 8.22 us -> 11.8 us
  transfers between devices with their start and end apart: 4 -> 0, of which waited for: 2 -> 0; matrix products, arithmetic and copies ran while one was open for 25% -> 0% of each run, Pallas kernels for 0% -> 0%
where the time goes in v1:
time: 61.8 us; the launch traced here: 60.7 us
  Pallas kernels  47.5 us (77%)
  local copies, waits for them, and re-layouts  13.1 us (21%)
    pallas_call x1, Pallas kernels, per_device(): pl.pallas_call(functools.partial(kernel, chips, cap, top), out_shape=jax....  47.5 us
    unnamed x7, local copies, waits for them, and re-layouts  11.8 us
    reshape x1, local copies, waits for them, and re-layouts, per_device(): aid.reshape(chips, 2 * rows)  1.36 us

profile of v1, /device:TPU:0, one launch (start us, length us, event | category | flops | bytes accessed | tf_op | source)
XLA Modules:
  0.0 60.7 jit_solution(188752240042814689)
XLA Ops:
  0.0 1.4 %copy.10.idx_ref = s32[16,6]{1,0:T(8,128)} copy(s32[16,6]{0,1:T(8,128)} %param.10) | data formatting | bytes 768 | tf_op args[1]
  1.4 1.4 %copy.11.gate_ref = f32[16,6]{1,0:T(8,128)} copy(f32[16,6]{0,1:T(8,128)} %param.11) | data formatting | bytes 768 | tf_op args[2]
  2.7 1.4 %reshape.3.aid_ref = s32[16,32]{1,0:T(8,128)} reshape(s32[512]{0:T(512)} %param.12) | data formatting | bytes 4096 | tf_op jit(solution)/shard_map/reshape | solution.py:308
  4.1 0.0 copy-start
  4.1 4.7 %copy.12.wg_hbm = bf16[1,2048,704]{2,1,0:T(8,128)(2,1)} copy(bf16[1,2048,704]{1,2,0:T(8,128)(2,1)} %param.13) | data formatting | bytes 5767168 | tf_op args[4]
  8.8 0.0 copy-done
  8.8 2.8 %copy.13.wu_hbm = bf16[1,2048,704]{2,1,0:T(8,128)(2,1)} copy(bf16[1,2048,704]{1,2,0:T(8,128)(2,1)S(1)} %copy-done) | data formatting | bytes 5767168 | tf_op args[5]
  11.7 47.5 %shard_map.91 = bf16[16,2048]{1,0:T(8,128)(2,1)} custom-call(bf16[16,2048]{1,0:T(8,128)(2,1)} %x_ref.1, s32[16,6]{1,0:T(8,128)} %copy.10.idx_ref, f32[16,6]{1,0:T(8,128)} %copy.11.gate_ref, s32[16,32]{1,0:T(8,128)} %reshape.3.aid_ref, bf16[1,2048,704]{2,1,0:T(8,128)(2,1)} %copy.12.wg_hbm, bf16[1,2048,704]{2,1,0:T(8,128)(2,1)} %copy.13.wu_hbm, ...), custom_call_target="tpu_custom_call" | custom-call | tf_op jit(solution)/shard_map/pallas_call | solution.py:286
  59.2 1.5 %copy.15 = bf16[16,2048]{1,0:T(8,128)(2,1)} copy(bf16[16,2048]{1,0:T(8,128)(2,1)} %shard_map.91) | data formatting | bytes 131072
Async XLA Ops:
  4.1 4.8 %copy-start = (bf16[1,2048,704]{1,2,0:T(8,128)(2,1)S(1)}, bf16[1,2048,704]{1,2,0:T(8,128)(2,1)}, u32[]{:S(2)}) copy-start(bf16[1,2048,704]{1,2,0:T(8,128)(2,1)} %param.14) | copy-start | bytes 8650756

commit v2 on v1

v2 whole, which is shorter than its diff:
```python
import functools

import jax
import jax.numpy as jnp
from jax import lax
from jax.experimental import pallas as pl
from jax.experimental.pallas import tpu as pltpu
from jax.sharding import PartitionSpec as P

RANK = 16
LANES = 128
BF16 = jnp.bfloat16
F32 = jnp.float32
MESH = pl.DeviceIdType.MESH


def dot_nt(a, b):
    return lax.dot_general(a, b, (((1,), (1,)), ((), ())), preferred_element_type=F32)


def kernel(
    chips, cap, top, x_ref, idx_ref, gate_ref, aid_ref, wg_hbm, wu_hbm, wd_hbm, adn_hbm, aup_hbm, out_ref,
    wg, wu, wd, adn, aup, col, disp, recv_a, recv_b, xs, hid, y_own, sib_send, sib_recv,
    rs_send, rs_recv, ag, cor_send, cor_recv, ret_send, ret_recv, low,
    w_sem, adl_sem, ad_s, ad_r, col_s, col_r, disp_s, disp_r, fwd_s, fwd_r, rs_s, rs_r,
    ag_s, ag_r, cor_s, cor_r, ret_s, ret_r, sib_s, sib_r,
):
    me = lax.axis_index("exp")
    q = lax.div(me, 2)
    c = lax.rem(me, 2)
    sib = me + 1 - 2 * c
    rows, width = x_ref.shape
    feats = adn_hbm.shape[0]
    bank = adn_hbm.shape[1]
    group = chips * rows
    slots = chips * cap
    parts, wide_n = y_own.shape[0], y_own.shape[2]
    off = pl.multiple_of(lax.rem(me * feats, LANES), feats)

    def remote(src, dst, ss, rs, dev):
        return pltpu.make_async_remote_copy(
            src_ref=src, dst_ref=dst, send_sem=ss, recv_sem=rs, device_id={"exp": dev}, device_id_type=MESH
        )

    def peer(r):
        return lax.rem(q + r, chips)

    def source(r):
        return lax.rem(q + chips - r, chips)

    def others(fn, first=1, last=chips):
        def step(r, carry):
            fn(r)
            return carry

        lax.fori_loop(first, last, step, 0)

    barrier = pltpu.get_barrier_semaphore()
    if 2 * feats < LANES:
        adn[...] = jnp.zeros_like(adn)
        aup[...] = jnp.zeros_like(aup)
    others(lambda r: pl.semaphore_signal(barrier, inc=1, device_id={"exp": 2 * peer(r) + c}, device_id_type=MESH))
    pl.semaphore_signal(barrier, inc=1, device_id={"exp": sib}, device_id_type=MESH)

    own_rows = pl.ds(off, feats)
    local = [
        pltpu.make_async_copy(adn_hbm, adn.at[own_rows], adl_sem.at[0]),
        pltpu.make_async_copy(wg_hbm.at[0], wg, w_sem.at[0]),
        pltpu.make_async_copy(wu_hbm.at[0], wu, w_sem.at[1]),
        pltpu.make_async_copy(aup_hbm, aup.at[own_rows], adl_sem.at[1]),
        pltpu.make_async_copy(wd_hbm.at[0], wd, w_sem.at[2]),
    ]
    for cp in local:
        cp.start()

    slot = lax.broadcasted_iota(jnp.int32, (slots, rows), 0)
    slot_e = lax.div(slot, cap)
    chosen = jnp.zeros((slots, rows), F32)
    weight = jnp.zeros((slots, rows), F32)
    for k in range(top):
        hit = idx_ref[k : k + 1, :] == slot_e
        chosen = chosen + jnp.where(hit, 1.0, 0.0)
        weight = weight + jnp.where(hit, gate_ref[k : k + 1, :], 0.0)
    earlier = jnp.where(
        lax.broadcasted_iota(jnp.int32, (rows, rows), 0) < lax.broadcasted_iota(jnp.int32, (rows, rows), 1), 1.0, 0.0
    )
    rank_of = jnp.dot(chosen.astype(BF16), earlier.astype(BF16), preferred_element_type=F32)
    slot_p = lax.rem(slot, cap).astype(F32)
    pick = jnp.where((chosen > 0.5) & (rank_of == slot_p), 1.0, 0.0)
    packed = jnp.dot(pick.astype(BF16), x_ref[...], preferred_element_type=F32)
    disp[...] = packed.reshape(chips, cap, width).astype(BF16)
    recv_a[pl.ds(q, 1)] = disp[pl.ds(q, 1)]

    def lanes_of(chip):
        return pl.ds(pl.multiple_of(lax.div(chip * 2 * feats, LANES) * LANES, LANES), LANES)

    col[pl.ds(q, 1)] = x_ref[:, lanes_of(q)].reshape(1, rows, LANES)

    pl.semaphore_wait(barrier, chips)

    def col_copy(to, slot):
        return remote(x_ref.at[:, lanes_of(to)], col.at[slot], col_s.at[to], col_r.at[slot], 2 * to + c)

    def disp_copy(to, slot):
        return remote(disp.at[to], recv_a.at[slot], disp_s.at[to], disp_r.at[slot], 2 * to + c)

    def fwd_copy(block):
        return remote(recv_a.at[block], recv_b.at[block], fwd_s.at[block], fwd_r.at[block], sib)

    def rs_copy(to, slot):
        return remote(rs_send.at[to], rs_recv.at[slot], rs_s.at[to], rs_r.at[slot], 2 * to + c)

    def ag_copy(to, slot):
        return remote(low, ag.at[slot], ag_s.at[to], ag_r.at[slot], 2 * to + c)

    def cor_copy(to, slot):
        return remote(cor_send.at[to], cor_recv.at[slot], cor_s.at[to], cor_r.at[slot], 2 * to + c)

    def ret_copy(j, to, slot):
        return remote(
            ret_send.at[j, to], ret_recv.at[j, slot], ret_s.at[j * chips + to], ret_r.at[j * chips + slot], 2 * to + c
        )

    def sib_copy(j):
        return remote(sib_send.at[j], sib_recv.at[j], sib_s.at[j], sib_r.at[j], sib)

    others(lambda r: col_copy(peer(r), q).start())
    adn_copy = remote(adn_hbm, adn.at[own_rows], ad_s.at[0], ad_r.at[0], sib)
    aup_copy = remote(aup_hbm, aup.at[own_rows], ad_s.at[1], ad_r.at[1], sib)
    adn_copy.start()
    early = 1 + (chips - 1) * 5 // 8
    others(lambda r: disp_copy(peer(r), q).start(), 1, early)
    aup_copy.start()
    fwd_copy(q).start()

    piece = 8 * LANES // (2 * rows)
    ids = []
    for first in range(0, chips, piece):
        n = min(piece, chips - first)
        part = lax.broadcasted_iota(jnp.int32, (n * rows, n * 2 * rows), 1)
        row = lax.broadcasted_iota(jnp.int32, (n * rows, n * 2 * rows), 0)
        here = lax.div(row, rows) * (2 * rows) + lax.rem(row, rows) + c * rows
        values = aid_ref[:, first * 2 * rows : (first + n) * 2 * rows].astype(F32)
        ids.append(jnp.sum(jnp.where(part == here, values, 0.0), axis=1, keepdims=True))
    ids = jnp.concatenate(ids, axis=0) if len(ids) > 1 else ids[0]
    ids = jnp.broadcast_to(ids, (group, LANES)).astype(jnp.int32)
    per = LANES // RANK
    id_hi = lax.div(ids, per)
    id_lo = ids - id_hi * per
    lane_g = lax.broadcasted_iota(jnp.int32, (group, LANES), 1)
    keep = lax.div(lane_g, RANK) == id_lo

    others(lambda r: col_copy(q, source(r)).wait_recv())
    local[0].wait()
    adn_copy.wait_recv()
    cols = col[...].reshape(group, LANES)
    span = 512
    sub = span // LANES

    def down_step(i, acc):
        at = pl.multiple_of(i * span, span)
        h = jnp.dot(cols, adn[:, pl.ds(at, span)], preferred_element_type=F32)
        for s in range(sub):
            acc = jnp.where(id_hi == i * sub + s, h[:, s * LANES : (s + 1) * LANES], acc)
        return acc

    terms = lax.fori_loop(0, bank // span, down_step, jnp.zeros((group, LANES), F32))
    terms = jnp.where(keep, terms, 0.0).astype(BF16)
    fi = lax.broadcasted_iota(jnp.int32, (LANES, LANES), 0)
    fj = lax.broadcasted_iota(jnp.int32, (LANES, LANES), 1)
    fold = jnp.where(lax.rem(fi, RANK) == lax.rem(fj, RANK), 1.0, 0.0).astype(BF16)
    turn = lax.div(lane_g, RANK) == lax.rem(lax.broadcasted_iota(jnp.int32, (group, LANES), 0), per)
    folded = jnp.where(turn, jnp.dot(terms, fold, preferred_element_type=F32), 0.0)
    rs_send[...] = jnp.sum(folded.reshape(group // per, per, LANES), axis=1).reshape(chips, rows // per, LANES)
    rs_recv[pl.ds(q, 1)] = rs_send[pl.ds(q, 1)]
    others(lambda r: rs_copy(peer(r), q).start())

    others(lambda r: disp_copy(peer(r), q).start(), early, chips)

    def forward(r):
        disp_copy(q, source(r)).wait_recv()
        fwd_copy(source(r)).start()

    others(forward, 1, early)
    others(lambda r: rs_copy(q, source(r)).wait_recv())
    low[...] = jnp.sum(rs_recv[...], axis=0).astype(BF16).astype(F32)
    ag[pl.ds(q, 1)] = low[...].reshape(1, rows // per, LANES)
    others(lambda r: ag_copy(peer(r), q).start())
    others(forward, early, chips)

    half = wd.shape[0]
    xs[:slots] = recv_a[...].astype(F32).reshape(slots, width).astype(BF16)
    local[1].wait()
    local[2].wait()
    local[4].wait()
    fwd_copy(q).wait_recv()
    others(lambda r: fwd_copy(source(r)).wait_recv())
    xs[slots:] = recv_b[...].astype(F32).reshape(slots, width).astype(BF16)
    cut = -(-half // (2 * LANES)) * LANES
    for a, b in ((0, cut), (cut, half)):
        g = dot_nt(wg[a:b], xs[...])
        u = dot_nt(wu[a:b], xs[...])
        hid[:, a:b] = (g / (1.0 + jnp.exp(-g)) * u).T.astype(BF16)

    def finish(j):
        sib_copy(j).wait_recv()
        ret_send[j] = (y_own[j].reshape(chips, cap, wide_n) + sib_recv[j].astype(F32)).astype(BF16)
        ret_recv[j, pl.ds(q, 1)] = ret_send[j, pl.ds(q, 1)]
        others(lambda r: ret_copy(j, peer(r), q).start())

    for j in range(parts):
        y = jnp.dot(hid[...], wd[:, j * wide_n : (j + 1) * wide_n], preferred_element_type=F32)
        sib_send[j] = y[slots:].reshape(chips, cap, wide_n).astype(BF16)
        sib_copy(j).start()
        y_own[j] = y[:slots]
        if j > 0:
            finish(j - 1)
    finish(parts - 1)

    others(lambda r: ag_copy(q, source(r)).wait_recv())
    local[3].wait()
    aup_copy.wait_recv()
    ranks = jnp.broadcast_to(ag[...].reshape(group // per, 1, LANES), (group // per, per, LANES)).reshape(group, LANES)
    ranks = jnp.where(turn, ranks, 0.0).astype(BF16)
    ranks = jnp.where(keep, jnp.dot(ranks, fold, preferred_element_type=F32), 0.0)

    def up_step(i, acc):
        at = pl.multiple_of(i * span, span)
        wide = jnp.concatenate([jnp.where(id_hi == i * sub + s, ranks, 0.0).astype(BF16) for s in range(sub)], axis=1)
        return acc + dot_nt(wide, aup[:, pl.ds(at, span)])

    corr = lax.fori_loop(0, bank // span, up_step, jnp.zeros((group, LANES), F32))
    cor_send[...] = corr.astype(BF16).reshape(chips, rows, LANES)
    cor_recv[pl.ds(q, 1)] = cor_send[pl.ds(q, 1)]
    others(lambda r: cor_copy(peer(r), q).start())

    others(lambda r: cor_copy(q, source(r)).wait_recv())
    combine = (pick * weight).T
    c_hi = combine.astype(BF16)
    c_lo = (combine - c_hi.astype(F32)).astype(BF16)
    share = LANES // (2 * feats)
    for j in range(parts):
        others(lambda r: ret_copy(j, q, source(r)).wait_recv())
        back = ret_recv[j].astype(F32).reshape(slots, wide_n).astype(BF16)
        routed = jnp.dot(c_hi, back, preferred_element_type=F32) + jnp.dot(c_lo, back, preferred_element_type=F32)
        for i in range(wide_n // LANES):
            first = (j * wide_n // LANES + i) * share
            delta = cor_recv[first].astype(F32)
            for s in range(1, share):
                delta = delta + cor_recv[first + s].astype(F32)
            out_ref[:, j * wide_n + i * LANES : j * wide_n + (i + 1) * LANES] = (
                routed[:, i * LANES : (i + 1) * LANES] + delta
            ).astype(BF16)

    adn_copy.wait_send()
    aup_copy.wait_send()
    for j in range(parts):
        sib_copy(j).wait_send()
    fwd_copy(q).wait_send()

    def drain(r):
        to = peer(r)
        for cp in (col_copy, disp_copy, rs_copy, ag_copy, cor_copy):
            cp(to, q).wait_send()
        for j in range(parts):
            ret_copy(j, to, q).wait_send()
        fwd_copy(source(r)).wait_send()

    others(drain)


def per_device(tokens, idx, gates, aid, wg, wu, wd, adn, aup):
    devices = lax.axis_size("exp")
    chips = devices // 2
    rows, width = tokens.shape
    top = idx.shape[1]
    half = wd.shape[1]
    feats, bank = adn.shape
    need = 2 * (rows * top // devices + 1)
    cap = -(-need // 8) * 8
    slots = chips * cap
    short = rows * RANK // LANES
    parts = 4
    wide_n = width // parts
    blocks = lambda *s: pltpu.VMEM(s, BF16)
    sems = lambda n: pltpu.SemaphoreType.DMA((n,))
    vm = pl.BlockSpec(memory_space=pltpu.VMEM)
    hbm = pl.BlockSpec(memory_space=pl.ANY)
    return pl.pallas_call(
        functools.partial(kernel, chips, cap, top),
        out_shape=jax.ShapeDtypeStruct((rows, width), BF16),
        in_specs=[vm, vm, vm, vm, hbm, hbm, hbm, hbm, hbm],
        out_specs=vm,
        scratch_shapes=[
            blocks(half, width), blocks(half, width), blocks(half, width),
            blocks(LANES, bank), blocks(LANES, bank),
            blocks(chips, rows, LANES),
            blocks(chips, cap, width), blocks(chips, cap, width), blocks(chips, cap, width),
            blocks(2 * slots, width), blocks(2 * slots, half), pltpu.VMEM((parts, slots, wide_n), F32),
            blocks(parts, chips, cap, wide_n), blocks(parts, chips, cap, wide_n),
            pltpu.VMEM((chips, short, LANES), F32), pltpu.VMEM((chips, short, LANES), F32),
            pltpu.VMEM((chips, short, LANES), F32),
            blocks(chips, rows, LANES), blocks(chips, rows, LANES),
            blocks(parts, chips, cap, wide_n), blocks(parts, chips, cap, wide_n), pltpu.VMEM((short, LANES), F32),
            sems(3), sems(2), sems(2), sems(2),
            *[sems(chips) for _ in range(12)],
            sems(parts * chips), sems(parts * chips), sems(parts), sems(parts),
        ],
        compiler_params=pltpu.CompilerParams(
            collective_id=0, has_side_effects=True, vmem_limit_bytes=60 * 1024 * 1024
        ),
    )(tokens, idx.T, gates.T, aid.reshape(1, -1), wg.swapaxes(1, 2), wu.swapaxes(1, 2), wd, adn, aup)


def solution(mesh):
    placed = (
        P(("grp", "exp"), None),
        P(("grp", "exp"), None),
        P(("grp", "exp"), None),
        P("grp"),
        P("exp", None, None),
        P("exp", None, None),
        P("exp", None, None),
        P("exp", None),
        P("exp", None),
    )
    return jax.shard_map(
        per_device, mesh=mesh, in_specs=placed, out_specs=P(("grp", "exp"), None), check_vma=False
    )
```

time: 61.8 us -> 49.1 us (0.79); the launches traced: 60.7 us -> 48.9 us
  local copies, waits for them, and re-layouts: 13.1 us -> 1.47 us
    unnamed x7 -> x1, local copies, waits for them, and re-layouts: 11.8 us -> 1.47 us
    reshape x1 -> x0, local copies, waits for them, and re-layouts: 1.36 us -> none  [per_device(): aid.reshape(chips, 2 * rows)]
where the time goes in v2:
time: 49.1 us; the launch traced here: 48.9 us
  Pallas kernels  47.4 us (97%)
  local copies, waits for them, and re-layouts  1.47 us (3%)
    pallas_call x1, Pallas kernels, per_device(): pl.pallas_call(functools.partial(kernel, chips, cap, top), out_shape=jax....  47.4 us
    unnamed x1, local copies, waits for them, and re-layouts  1.47 us

profile of v2, /device:TPU:0, one launch (start us, length us, event | category | flops | bytes accessed | tf_op | source)
XLA Modules:
  0.0 48.9 jit_solution(17272089415678940711)
XLA Ops:
  0.0 47.4 %shard_map.91 = bf16[16,2048]{1,0:T(8,128)(2,1)} custom-call(bf16[16,2048]{1,0:T(8,128)(2,1)} %x_ref.1, s32[6,16]{1,0:T(8,128)} %bitcast.7, f32[6,16]{1,0:T(8,128)} %bitcast.8, s32[1,512]{1,0:T(1,128)} %bitcast.9, bf16[1,704,2048]{2,1,0:T(8,128)(2,1)} %bitcast.5, bf16[1,704,2048]{2,1,0:T(8,128)(2,1)} %bitcast.6, bf16[1,704,2048]{2,1,0:T(8,128)(2,1)} %wd_hbm.1, ...), custom_call_target="tpu_custom_call" | custom-call | tf_op jit(solution)/shard_map/pallas_call | solution.py:289
  47.4 1.5 %copy.11 = bf16[16,2048]{1,0:T(8,128)(2,1)} copy(bf16[16,2048]{1,0:T(8,128)(2,1)} %shard_map.91) | data formatting | bytes 131072
